TPU v7x, 32 devices: a whole 2x2x4 slice. The times are simulated.
32 devices in a mesh: row: 4 (over x, core), col: 8 (over z, y).
Axes of the slice: x: 2, y: 2, z: 4, core: 2. Of those that a mesh axis runs over, the one named last changes fastest.
Arguments:
- matrix: float32 [2048, 2048], P('row', 'col'), as said below
- start_vectors: float32 [2048, 512], P(('col', 'row')), may hold values from -6 to 6
- interval: float32 [2], replicated, as said below
Outputs:
- ortho_basis: float32 [2048, 512], P(('col', 'row'))
- projected: float32 [512, 512], replicated
- residual: float32 [2048, 512], P(('col', 'row'))
Inputs may be any that keep to these rules, and one draw needn't show every extreme that they name: matrix is exactly symmetric (entry (r, c) equals entry (c, r)); its eigenvalues lie within about -1.45 to 1.45. interval[0] lies in [-1.2, -0.7] and interval[1] in [1.45, 1.9].
All inputs are finite; a program needn't handle non-finite values.
Results may differ from a plain program's by a relative error of at most 0.0003.
Values sent between devices are 32-bit elements.
A program may use at most 128 MiB of HBM per device.

v0:
```python
import jax
import jax.numpy as jnp
from jax import lax
from jax.sharding import PartitionSpec as P

FILTER_DEG = 3
OUTER = 2


def scattered(contribution, width, axis):
    whole = contribution(jnp.int32(0), width * lax.axis_size(axis))
    return lax.psum_scatter(whole, axis, scatter_dimension=0, tiled=True)


def spread(array, axis, root):
    mine = lax.axis_index(axis) == root
    return lax.psum(jnp.where(mine, array, jnp.zeros_like(array)), axis)


def product(left, right):
    return jnp.dot(left, right, precision=lax.Precision.HIGHEST, preferred_element_type=jnp.float32)


def tri_solve(factor, values):
    return jax.scipy.linalg.solve_triangular(factor, values, lower=True)


def on_device(matrix, start_vectors, interval):
    block_rows, block_cols = matrix.shape
    slab_rows = start_vectors.shape[0]
    total_rows = slab_rows * lax.axis_size("row") * lax.axis_size("col")
    row_index = lax.axis_index("row")
    col_index = lax.axis_index("col")
    center = 0.5 * (interval[0] + interval[1])
    half_width = 0.5 * (interval[1] - interval[0])
    global_rows = row_index * block_rows + lax.iota(jnp.int32, block_rows)
    global_cols = col_index * block_cols + lax.iota(jnp.int32, block_cols)
    diagonal = global_rows[:, None] == global_cols[None, :]
    shifted = jnp.where(diagonal, matrix - center, matrix) / half_width

    def forward(col_full):

        def term(first_row, row_count):
            strip = lax.dynamic_slice_in_dim(shifted, first_row, row_count, 0)
            return product(strip, col_full)

        return scattered(term, slab_rows, "col")

    def gather_rows(slab_part):
        return lax.all_gather(slab_part, "col", axis=0, tiled=True)

    def to_columns(row_full):
        root_row = col_index * block_cols // block_rows
        offset = col_index * block_cols - root_row * block_rows
        column_part = lax.dynamic_slice_in_dim(row_full, offset, block_cols, 0)
        return spread(column_part, "row", root_row)

    def backward(row_full):
        partial_value = lax.dot_general(
            shifted,
            row_full,
            (((0,), (0,)), ((), ())),
            precision=lax.Precision.HIGHEST,
            preferred_element_type=jnp.float32,
        )
        return lax.psum(partial_value, "row")

    current_start = lax.all_gather(start_vectors, "row", axis=0, tiled=True)
    for sweep_index in range(OUTER):
        even_cols = current_start
        odd_slab = forward(current_start)
        odd_rows = gather_rows(odd_slab)
        for degree in range(2, FILTER_DEG + 1):
            if degree % 2 == 0:
                even_cols = 2.0 * backward(odd_rows) - even_cols
            else:
                odd_slab = 2.0 * forward(even_cols) - odd_slab
                odd_rows = gather_rows(odd_slab)
        final_cols = to_columns(odd_rows)
        mapped_cols = backward(odd_rows)
        final_slab = lax.dynamic_slice_in_dim(final_cols, row_index * slab_rows, slab_rows, 0)
        mapped_slab = lax.dynamic_slice_in_dim(mapped_cols, row_index * slab_rows, slab_rows, 0)
        gram_part = product(final_slab.T, final_slab)
        cross_part = product(final_slab.T, mapped_slab)
        gram_total = lax.psum(gram_part, ("row", "col"))
        cross_total = lax.psum(cross_part, ("row", "col"))
        gram_matrix = gram_total / total_rows
        cross_terms = cross_total / total_rows
        factor = jnp.linalg.cholesky(gram_matrix)
        basis_cols = tri_solve(factor, final_cols.T).T
        partial_proj = tri_solve(factor, cross_terms)
        projected = tri_solve(factor, partial_proj.T).T
        current_start = basis_cols
    basis_slab = lax.dynamic_slice_in_dim(current_start, row_index * slab_rows, slab_rows, 0)
    residual = tri_solve(factor, mapped_slab.T).T - product(basis_slab, projected)
    return (basis_slab, projected, residual)


def solution(mesh):
    return jax.shard_map(
        on_device,
        mesh=mesh,
        in_specs=(P("row", "col"), P(("col", "row"), None), P()),
        out_specs=(P(("col", "row"), None), P(), P(("col", "row"), None)),
        check_vma=False,
    )
```

profile of v0, /device:TPU:0, one launch (start us, length us, event | category | flops | bytes accessed | tf_op | source)
XLA Modules:
  0.0 1179.7 jit_solution(1612085924572650123)
XLA Ops:
  11.0 8.9 all_gather.15
  22.0 65.1 %reduce-scatter.5.cloned.1.call-done = f32[64,512]{1,0:T(8,128)} async-done(((f32[512,512]{1,0:T(8,128)}), f32[64,512]{1,0:T(8,128)}) %reduce-scatter.5.cloned.1.call-update) | async-done | bytes 131088 | tf_op jit(solution)/shard_map/reduce_scatter | solution.py:12
  87.2 41.3 %all-gather.5.cloned.1.call-done = f32[512,512]{1,0:T(8,128)} async-done(((f32[64,512]{1,0:T(8,128)}), f32[512,512]{1,0:T(8,128)}) %all-gather.5.cloned.1.call-update) | async-done | bytes 1048592 | tf_op jit(solution)/shard_map/all_gather | solution.py:50
  132.7 32.0 %all-reduce.10.cloned.1.call-done = f32[256,512]{0,1:T(8,128)} async-done(((f32[256,512]{0,1:T(8,128)}), f32[256,512]{0,1:T(8,128)}) %all-reduce.10.cloned.1.call-update) | async-done | bytes 524304 | tf_op jit(solution)/shard_map/psum | solution.py:66
  167.9 65.6 %reduce-scatter.7.cloned.1.call-done = f32[64,512]{1,0:T(8,128)} async-done(((f32[512,512]{1,0:T(8,128)}), f32[64,512]{1,0:T(8,128)}) %reduce-scatter.7.cloned.1.call-update) | async-done | bytes 131088 | tf_op jit(solution)/shard_map/reduce_scatter | solution.py:12
  235.3 40.1 %all-gather.7.cloned.1.call-done = f32[512,512]{1,0:T(8,128)} async-done(((f32[64,512]{1,0:T(8,128)}), f32[512,512]{1,0:T(8,128)}) %all-gather.7.cloned.1.call-update) | async-done | bytes 1048592 | tf_op jit(solution)/shard_map/all_gather | solution.py:50
  277.3 33.0 %all-reduce.12.cloned.1.call-done = f32[256,512]{1,0:T(8,128)} async-done(((f32[256,512]{1,0:T(8,128)}), f32[256,512]{1,0:T(8,128)}) %all-reduce.12.cloned.1.call-update) | async-done | bytes 524304 | tf_op jit(solution)/shard_map/psum | solution.py:17
  313.5 133.4 %all-reduce.14.cloned.1.call-done = f32[512,512]{0,1:T(8,128)} async-done(((f32[512,512]{0,1:T(8,128)}), f32[512,512]{0,1:T(8,128)}) %all-reduce.14.cloned.1.call-update) | async-done | bytes 1048592 | tf_op jit(solution)/shard_map/psum | solution.py:85
  449.7 11.7 cholesky.286
  461.5 9.8 custom-call.36
  472.1 11.7 cholesky.305
  483.8 10.0 custom-call.37
  494.5 11.7 cholesky.326
  507.0 9.8 custom-call.38
  517.4 11.7 cholesky.343
  533.6 8.5 while.9
  542.1 39.3 %custom-call.39 = f32[4,128,128]{1,2,0:T(8,128)S(1)} custom-call(f32[4,128,128]{2,1,0:T(8,128)S(1)} %get-tuple-element.42), custom_call_target="InvertDiagBlocksLowerTriangular" | custom-call | tf_op jit(solution)/shard_map/jit(_solve_triangular)/triangular_solve | solution.py:25
  586.6 63.4 %reduce-scatter.9.cloned.1.call-done = f32[64,512]{1,0:T(8,128)} async-done(((f32[512,512]{1,0:T(8,128)}), f32[64,512]{1,0:T(8,128)}) %reduce-scatter.9.cloned.1.call-update) | async-done | bytes 131088 | tf_op jit(solution)/shard_map/reduce_scatter | solution.py:12
  650.1 41.3 %all-gather.9.cloned.1.call-done = f32[512,512]{1,0:T(8,128)} async-done(((f32[64,512]{1,0:T(8,128)}), f32[512,512]{1,0:T(8,128)}) %all-gather.9.cloned.1.call-update) | async-done | bytes 1048592 | tf_op jit(solution)/shard_map/all_gather | solution.py:50
  695.4 32.2 %all-reduce.16.cloned.1.call-done = f32[256,512]{0,1:T(8,128)} async-done(((f32[256,512]{0,1:T(8,128)}), f32[256,512]{0,1:T(8,128)}) %all-reduce.16.cloned.1.call-update) | async-done | bytes 524304 | tf_op jit(solution)/shard_map/psum | solution.py:66
  730.8 65.8 %reduce-scatter.11.cloned.1.call-done = f32[64,512]{1,0:T(8,128)} async-done(((f32[512,512]{1,0:T(8,128)}), f32[64,512]{1,0:T(8,128)}) %reduce-scatter.11.cloned.1.call-update) | async-done | bytes 131088 | tf_op jit(solution)/shard_map/reduce_scatter | solution.py:12
  798.2 40.2 %all-gather.11.cloned.1.call-done = f32[512,512]{1,0:T(8,128)} async-done(((f32[64,512]{1,0:T(8,128)}), f32[512,512]{1,0:T(8,128)}) %all-gather.11.cloned.1.call-update) | async-done | bytes 1048592 | tf_op jit(solution)/shard_map/all_gather | solution.py:50
  842.8 35.0 %all-reduce.20.cloned.1.call-done = (f32[256,512]{1,0:T(8,128)}, f32[256,512]{1,0:T(8,128)}) async-done(((f32[256,512]{1,0:T(8,128)}, f32[256,512]{1,0:T(8,128)}), (f32[256,512]{1,0:T(8,128)}, f32[256,512]{1,0:T(8,128)})) %all-reduce.20.cloned.1.call-update) | async-done | bytes 1048592 | tf_op jit(solution)/shard_map/psum | solution.py:17
  883.7 135.3 %all-reduce.18.cloned.1.call-done = (f32[512,512]{0,1:T(8,128)}, f32[512,512]{0,1:T(8,128)}) async-done(((f32[512,512]{0,1:T(8,128)}, f32[512,512]{0,1:T(8,128)}), (f32[512,512]{0,1:T(8,128)}, f32[512,512]{0,1:T(8,128)})) %all-reduce.18.cloned.1.call-update) | async-done | bytes 2097168 | tf_op jit(solution)/shard_map/psum | solution.py:85
  1022.1 11.7 cholesky.358
  1034.5 9.8 custom-call.40
  1045.1 12.1 %cholesky.377 = f32[128,128]{1,0:T(8,128)S(1)} custom-call(f32[128,128]{1,0:T(8,128)S(1)} %cholesky.443), custom_call_target="Cholesky" | custom-call | tf_op jit(solution)/shard_map/jit(cholesky)/cholesky | solution.py:89
  1057.9 9.8 custom-call.41
  1068.4 11.7 cholesky.398
  1080.8 9.8 custom-call.42
  1091.2 11.7 cholesky.415
  1114.8 39.5 %custom-call.43 = f32[4,128,128]{1,2,0:T(8,128)S(1)} custom-call(f32[4,128,128]{2,1,0:T(8,128)S(1)} %get-tuple-element.43), custom_call_target="InvertDiagBlocksLowerTriangular" | custom-call | tf_op jit(solution)/shard_map/jit(_solve_triangular)/triangular_solve | solution.py:25
  (185 shorter events, 101.1 us)
Async XLA Ops:
  7.2 0.7 copy-start.9
  7.2 12.7 %copy-start.10 = (f32[512,256]{1,0:T(8,128)S(1)}, f32[512,256]{1,0:T(8,128)}, u32[]{:S(2)}) copy-start(f32[512,256]{1,0:T(8,128)} %param.8) | copy-start | bytes 1572868
  7.2 80.0 %reduce-scatter.5.cloned.1.call-start = ((), (), s32[]{:S(2)}) async-start(), calls=%async_computation.4 | async-start | bytes 1179648 | tf_op jit(solution)/shard_map/reduce_scatter | solution.py:12
  22.0 106.6 %all-gather.5.cloned.1.call-start = ((), (), s32[]{:S(2)}) async-start(), calls=%async_computation.5 | async-start | bytes 1179648 | tf_op jit(solution)/shard_map/all_gather | solution.py:50
  87.2 77.6 %all-reduce.10.cloned.1.call-start = ((), (), s32[]{:S(2)}) async-start(), calls=%async_computation.6 | async-start | bytes 1048576 | tf_op jit(solution)/shard_map/psum | solution.py:66
  132.5 101.1 %reduce-scatter.7.cloned.1.call-start = ((), (), s32[]{:S(2)}) async-start(), calls=%async_computation.7 | async-start | bytes 1179648 | tf_op jit(solution)/shard_map/reduce_scatter | solution.py:12
  167.9 65.7 %copy-start.6 = (f32[64,512]{1,0:T(8,128)S(1)}, f32[64,512]{1,0:T(8,128)}, u32[]{:S(2)}) copy-start(f32[64,512]{1,0:T(8,128)} %reduce-scatter.5.cloned.1.call-done) | copy-start | bytes 393220
  167.9 107.5 %all-gather.7.cloned.1.call-start = ((), (), s32[]{:S(2)}) async-start(), calls=%async_computation.8 | async-start | bytes 1179648 | tf_op jit(solution)/shard_map/all_gather | solution.py:50
  235.2 75.1 %all-reduce.12.cloned.1.call-start = ((), (), s32[]{:S(2)}) async-start(), calls=%async_computation.9 | async-start | bytes 1048576 | tf_op jit(solution)/shard_map/psum | solution.py:17
  277.3 169.7 %all-reduce.14.cloned.1.call-start = ((), (), s32[]{:S(2)}) async-start(), calls=%async_computation.10 | async-start | bytes 2097152 | tf_op jit(solution)/shard_map/psum | solution.py:85
  313.3 336.7 %reduce-scatter.9.cloned.1.call-start = ((), (), s32[]{:S(2)}) async-start(), calls=%async_computation.11 | async-start | bytes 1179648 | tf_op jit(solution)/shard_map/reduce_scatter | solution.py:12
  448.3 1.2 copy-start.1
  533.4 48.0 %copy-start.4 = (f32[256,512]{1,0:T(8,128)S(1)}, f32[256,512]{1,0:T(8,128)}, u32[]{:S(2)}) copy-start(f32[256,512]{1,0:T(8,128)} %all-reduce.12.cloned.1.call-done) | copy-start | bytes 1572868
  583.3 1.2 copy-start.11
  586.6 104.8 %all-gather.9.cloned.1.call-start = ((), (), s32[]{:S(2)}) async-start(), calls=%async_computation.12 | async-start | bytes 1179648 | tf_op jit(solution)/shard_map/all_gather | solution.py:50
  650.0 77.6 %all-reduce.16.cloned.1.call-start = ((), (), s32[]{:S(2)}) async-start(), calls=%async_computation.13 | async-start | bytes 1048576 | tf_op jit(solution)/shard_map/psum | solution.py:66
  695.3 101.2 %reduce-scatter.11.cloned.1.call-start = ((), (), s32[]{:S(2)}) async-start(), calls=%async_computation.14 | async-start | bytes 1179648 | tf_op jit(solution)/shard_map/reduce_scatter | solution.py:12
  730.7 65.8 %copy-start.5 = (f32[64,512]{1,0:T(8,128)S(1)}, f32[64,512]{1,0:T(8,128)}, u32[]{:S(2)}) copy-start(f32[64,512]{1,0:T(8,128)} %reduce-scatter.9.cloned.1.call-done) | copy-start | bytes 393220
  730.7 107.6 %all-gather.11.cloned.1.call-start = ((), (), s32[]{:S(2)}) async-start(), calls=%async_computation.15 | async-start | bytes 1179648 | tf_op jit(solution)/shard_map/all_gather | solution.py:50
  798.2 79.6 %all-reduce.20.cloned.1.call-start = ((), (), s32[]{:S(2)}) async-start(), calls=%async_computation.17 | async-start | bytes 2097152 | tf_op jit(solution)/shard_map/psum | solution.py:17
  838.4 3.3 copy-start.7
  842.6 176.4 %all-reduce.18.cloned.1.call-start = ((), (), s32[]{:S(2)}) async-start(), calls=%async_computation.16 | async-start | bytes 4194304 | tf_op jit(solution)/shard_map/psum | solution.py:85
  877.8 3.0 copy-start.8
  1019.0 2.4 copy-start
  1154.7 1.3 copy-start.3
  1158.0 2.1 copy-start.2
Sparse Core Ops, SparseCore 0:
  22.1 65.0 reduce-scatter.4
  89.3 39.2 all-gather.4
  132.6 32.0 all-reduce.9
  168.6 64.9 reduce-scatter.6
  236.1 39.1 all-gather.6
  278.2 32.0 all-reduce.11
  316.1 130.8 all-reduce.13
  586.7 63.2 reduce-scatter.8
  652.1 39.2 all-gather.8
  695.4 32.1 all-reduce.15
  731.6 64.9 reduce-scatter.10
  799.1 39.2 all-gather.10
  842.7 35.0 all-reduce.19
  883.8 135.1 all-reduce.17
where the time goes:
time: 1190 us; the launch traced here: 1180 us
  waiting for transfers between devices  824 us (69%)
  other arithmetic  248 us (21%)
  matrix products  53.3 us (4%)
  between operations  22.6 us (2%)
  local copies, waits for them, and re-layouts  22.2 us (2%)
    psum x2, waiting for transfers between devices, on_device(): gram_total = lax.psum(gram_part, ('row', 'col'))  269 us
    reduce_scatter x4, waiting for transfers between devices, scattered(): return lax.psum_scatter(whole, axis, scatter_dimension=0, tiled=True)  260 us
    all_gather x4, waiting for transfers between devices, gather_rows(): return lax.all_gather(slab_part, 'col', axis=0, tiled=True)  163 us
    another operation x29, other arithmetic, on_device(): factor = jnp.linalg.cholesky(gram_matrix)  158 us
    another operation x6, other arithmetic, tri_solve(): return jax.scipy.linalg.solve_triangular(factor, values, lower=True)  79.2 us
    psum x2, waiting for transfers between devices, spread(): return lax.psum(jnp.where(mine, array, jnp.zeros_like(array)), axis)  67.9 us
    psum x2, waiting for transfers between devices, backward(): return lax.psum(partial_value, 'row')  64.2 us
  transfers between devices with their start and end apart: 14, of which 14 were waited for; matrix products, arithmetic and copies ran while one was open for 0% of the time, Pallas kernels for 0%

commit v1 on v0

--- a/solution.py
+++ b/solution.py
@@ -82,7 +82,7 @@
         mapped_slab = lax.dynamic_slice_in_dim(mapped_cols, row_index * slab_rows, slab_rows, 0)
         gram_part = product(final_slab.T, final_slab)
         cross_part = product(final_slab.T, mapped_slab)
-        gram_total = lax.psum(gram_part, ("row", "col"))
+        gram_total = lax.psum(lax.psum(gram_part, "col"), "row")
         cross_total = lax.psum(cross_part, ("row", "col"))
         gram_matrix = gram_total / total_rows
         cross_terms = cross_total / total_rows

time: 1190 us -> 1280 us (1.076)
  waiting for transfers between devices: 824 us -> 921 us
    psum x2 -> x5, waiting for transfers between devices: 269 us -> 366 us  [the longest x4 240 us: on_device(): gram_total = lax.psum(lax.psum(gram_part, 'col'), 'row')]
  transfers between devices with their start and end apart: 14 -> 17, of which waited for: 14 -> 17; matrix products, arithmetic and copies ran while one was open for 0% -> 1% of each run, Pallas kernels for 0% -> 0%
where the time goes in v1:
time: 1280 us
  waiting for transfers between devices  921 us (72%)
  other arithmetic  249 us (19%)
  matrix products  51 us (4%)
  local copies, waits for them, and re-layouts  22.6 us (2%)
  between operations  22.6 us (2%)
    reduce_scatter x4, waiting for transfers between devices, scattered(): return lax.psum_scatter(whole, axis, scatter_dimension=0, tiled=True)  261 us
    psum x4, waiting for transfers between devices, on_device(): gram_total = lax.psum(lax.psum(gram_part, 'col'), 'row')  240 us
    all_gather x4, waiting for transfers between devices, gather_rows(): return lax.all_gather(slab_part, 'col', axis=0, tiled=True)  163 us
    another operation x29, other arithmetic, on_device(): factor = jnp.linalg.cholesky(gram_matrix)  158 us
    psum x1, waiting for transfers between devices, on_device(): cross_total = lax.psum(cross_part, ('row', 'col'))  126 us
    another operation x6, other arithmetic, tri_solve(): return jax.scipy.linalg.solve_triangular(factor, values, lower=True)  79.2 us
    psum x2, waiting for transfers between devices, spread(): return lax.psum(jnp.where(mine, array, jnp.zeros_like(array)), axis)  65.9 us
    psum x2, waiting for transfers between devices, backward(): return lax.psum(partial_value, 'row')  64.2 us
  transfers between devices with their start and end apart: 17, of which 17 were waited for; matrix products, arithmetic and copies ran while one was open for 1% of the time, Pallas kernels for 0%

profile of v1, /device:TPU:0, one launch (start us, length us, event | category | flops | bytes accessed | tf_op | source)
XLA Modules:
  0.0 1275.9 jit_solution(11193210304757238607)
XLA Ops:
  22.0 65.2 %reduce-scatter.5.cloned.1.call-done = f32[64,512]{1,0:T(8,128)} async-done(((f32[512,512]{1,0:T(8,128)}), f32[64,512]{1,0:T(8,128)}) %reduce-scatter.5.cloned.1.call-update) | async-done | bytes 131088 | tf_op jit(solution)/shard_map/reduce_scatter | solution.py:12
  87.3 41.3 %all-gather.5.cloned.1.call-done = f32[512,512]{1,0:T(8,128)} async-done(((f32[64,512]{1,0:T(8,128)}), f32[512,512]{1,0:T(8,128)}) %all-gather.5.cloned.1.call-update) | async-done | bytes 1048592 | tf_op jit(solution)/shard_map/all_gather | solution.py:50
  132.8 32.0 %all-reduce.12.cloned.1.call-done = f32[256,512]{0,1:T(8,128)} async-done(((f32[256,512]{0,1:T(8,128)}), f32[256,512]{0,1:T(8,128)}) %all-reduce.12.cloned.1.call-update) | async-done | bytes 524304 | tf_op jit(solution)/shard_map/psum | solution.py:66
  168.0 65.6 %reduce-scatter.7.cloned.1.call-done = f32[64,512]{1,0:T(8,128)} async-done(((f32[512,512]{1,0:T(8,128)}), f32[64,512]{1,0:T(8,128)}) %reduce-scatter.7.cloned.1.call-update) | async-done | bytes 131088 | tf_op jit(solution)/shard_map/reduce_scatter | solution.py:12
  235.4 40.1 %all-gather.7.cloned.1.call-done = f32[512,512]{1,0:T(8,128)} async-done(((f32[64,512]{1,0:T(8,128)}), f32[512,512]{1,0:T(8,128)}) %all-gather.7.cloned.1.call-update) | async-done | bytes 1048592 | tf_op jit(solution)/shard_map/all_gather | solution.py:50
  277.4 33.0 %all-reduce.14.cloned.1.call-done = f32[256,512]{1,0:T(8,128)} async-done(((f32[256,512]{1,0:T(8,128)}), f32[256,512]{1,0:T(8,128)}) %all-reduce.14.cloned.1.call-update) | async-done | bytes 524304 | tf_op jit(solution)/shard_map/psum | solution.py:17
  313.4 79.5 %all-reduce.16.cloned.1.call-done = f32[512,512]{0,1:T(8,128)} async-done(((f32[512,512]{0,1:T(8,128)}), f32[512,512]{0,1:T(8,128)}) %all-reduce.16.cloned.1.call-update) | async-done | bytes 1048592 | tf_op jit(solution)/shard_map/psum | solution.py:85
  393.2 38.0 %all-reduce.18.cloned.1.call-done = f32[512,512]{0,1:T(8,128)} async-done(((f32[512,512]{0,1:T(8,128)}), f32[512,512]{0,1:T(8,128)}) %all-reduce.18.cloned.1.call-update) | async-done | bytes 1048592 | tf_op jit(solution)/shard_map/psum | solution.py:85
  434.0 11.7 cholesky.286
  445.9 9.8 custom-call.36
  456.4 11.7 cholesky.305
  468.1 10.0 custom-call.37
  478.8 11.7 cholesky.326
  491.3 9.8 custom-call.38
  501.7 11.7 cholesky.343
  526.4 39.3 %custom-call.39 = f32[4,128,128]{1,2,0:T(8,128)S(1)} custom-call(f32[4,128,128]{2,1,0:T(8,128)S(1)} %get-tuple-element.42), custom_call_target="InvertDiagBlocksLowerTriangular" | custom-call | tf_op jit(solution)/shard_map/jit(_solve_triangular)/triangular_solve | solution.py:25
  570.9 64.8 %reduce-scatter.9.cloned.1.call-done = f32[64,512]{1,0:T(8,128)} async-done(((f32[512,512]{1,0:T(8,128)}), f32[64,512]{1,0:T(8,128)}) %reduce-scatter.9.cloned.1.call-update) | async-done | bytes 131088 | tf_op jit(solution)/shard_map/reduce_scatter | solution.py:12
  635.8 41.2 %all-gather.9.cloned.1.call-done = f32[512,512]{1,0:T(8,128)} async-done(((f32[64,512]{1,0:T(8,128)}), f32[512,512]{1,0:T(8,128)}) %all-gather.9.cloned.1.call-update) | async-done | bytes 1048592 | tf_op jit(solution)/shard_map/all_gather | solution.py:50
  681.0 32.2 %all-reduce.20.cloned.1.call-done = f32[256,512]{0,1:T(8,128)} async-done(((f32[256,512]{0,1:T(8,128)}), f32[256,512]{0,1:T(8,128)}) %all-reduce.20.cloned.1.call-update) | async-done | bytes 524304 | tf_op jit(solution)/shard_map/psum | solution.py:66
  716.4 65.6 %reduce-scatter.11.cloned.1.call-done = f32[64,512]{1,0:T(8,128)} async-done(((f32[512,512]{1,0:T(8,128)}), f32[64,512]{1,0:T(8,128)}) %reduce-scatter.11.cloned.1.call-update) | async-done | bytes 131088 | tf_op jit(solution)/shard_map/reduce_scatter | solution.py:12
  783.7 40.3 %all-gather.11.cloned.1.call-done = f32[512,512]{1,0:T(8,128)} async-done(((f32[64,512]{1,0:T(8,128)}), f32[512,512]{1,0:T(8,128)}) %all-gather.11.cloned.1.call-update) | async-done | bytes 1048592 | tf_op jit(solution)/shard_map/all_gather | solution.py:50
  825.9 33.0 %all-reduce.22.cloned.1.call-done = f32[256,512]{1,0:T(8,128)} async-done(((f32[256,512]{1,0:T(8,128)}), f32[256,512]{1,0:T(8,128)}) %all-reduce.22.cloned.1.call-update) | async-done | bytes 524304 | tf_op jit(solution)/shard_map/psum | solution.py:17
  864.0 77.4 %all-reduce.24.cloned.1.call-done = f32[512,512]{0,1:T(8,128)} async-done(((f32[512,512]{0,1:T(8,128)}), f32[512,512]{0,1:T(8,128)}) %all-reduce.24.cloned.1.call-update) | async-done | bytes 1048592 | tf_op jit(solution)/shard_map/psum | solution.py:85
  941.6 44.6 %all-reduce.28.cloned.1.call-done = (f32[512,512]{0,1:T(8,128)}, f32[256,512]{1,0:T(8,128)}) async-done(((f32[512,512]{0,1:T(8,128)}, f32[256,512]{1,0:T(8,128)}), (f32[512,512]{0,1:T(8,128)}, f32[256,512]{1,0:T(8,128)})) %all-reduce.28.cloned.1.call-update) | async-done | bytes 1572880 | tf_op jit(solution)/shard_map/psum | solution.py:85
  989.0 11.7 cholesky.358
  1000.9 9.8 custom-call.40
  1011.4 11.7 cholesky.377
  1024.4 10.2 custom-call.41
  1035.3 11.7 cholesky.398
  1058.2 11.7 cholesky.415
  1081.3 39.5 %custom-call.43 = f32[4,128,128]{1,2,0:T(8,128)S(1)} custom-call(f32[4,128,128]{2,1,0:T(8,128)S(1)} %get-tuple-element.43), custom_call_target="InvertDiagBlocksLowerTriangular" | custom-call | tf_op jit(solution)/shard_map/jit(_solve_triangular)/triangular_solve | solution.py:25
  1128.5 126.4 %all-reduce.26.cloned.1.call-done = f32[512,512]{0,1:T(8,128)} async-done(((f32[512,512]{0,1:T(8,128)}), f32[512,512]{0,1:T(8,128)}) %all-reduce.26.cloned.1.call-update) | async-done | bytes 1048592 | tf_op jit(solution)/shard_map/psum | solution.py:86
  (192 shorter events, 127.2 us)
Async XLA Ops:
  7.2 0.7 copy-start.8
  7.2 12.7 copy-start.9
  7.2 80.1 %reduce-scatter.5.cloned.1.call-start = ((), (), s32[]{:S(2)}) async-start(), calls=%async_computation.4 | async-start | bytes 1179648 | tf_op jit(solution)/shard_map/reduce_scatter | solution.py:12
  22.0 106.6 %all-gather.5.cloned.1.call-start = ((), (), s32[]{:S(2)}) async-start(), calls=%async_computation.5 | async-start | bytes 1179648 | tf_op jit(solution)/shard_map/all_gather | solution.py:50
  87.3 77.6 %all-reduce.12.cloned.1.call-start = ((), (), s32[]{:S(2)}) async-start(), calls=%async_computation.6 | async-start | bytes 1048576 | tf_op jit(solution)/shard_map/psum | solution.py:66
  132.6 101.1 %reduce-scatter.7.cloned.1.call-start = ((), (), s32[]{:S(2)}) async-start(), calls=%async_computation.7 | async-start | bytes 1179648 | tf_op jit(solution)/shard_map/reduce_scatter | solution.py:12
  168.0 65.7 %copy-start.5 = (f32[64,512]{1,0:T(8,128)S(1)}, f32[64,512]{1,0:T(8,128)}, u32[]{:S(2)}) copy-start(f32[64,512]{1,0:T(8,128)} %reduce-scatter.5.cloned.1.call-done) | copy-start | bytes 393220
  168.0 107.5 %all-gather.7.cloned.1.call-start = ((), (), s32[]{:S(2)}) async-start(), calls=%async_computation.8 | async-start | bytes 1179648 | tf_op jit(solution)/shard_map/all_gather | solution.py:50
  235.3 75.1 %all-reduce.14.cloned.1.call-start = ((), (), s32[]{:S(2)}) async-start(), calls=%async_computation.9 | async-start | bytes 1048576 | tf_op jit(solution)/shard_map/psum | solution.py:17
  277.4 115.6 %all-reduce.16.cloned.1.call-start = ((), (), s32[]{:S(2)}) async-start(), calls=%async_computation.10 | async-start | bytes 2097152 | tf_op jit(solution)/shard_map/psum | solution.py:85
  313.4 117.8 %all-reduce.18.cloned.1.call-start = ((), (), s32[]{:S(2)}) async-start(), calls=%async_computation.11 | async-start | bytes 2097152 | tf_op jit(solution)/shard_map/psum | solution.py:85
  393.0 242.8 %reduce-scatter.9.cloned.1.call-start = ((), (), s32[]{:S(2)}) async-start(), calls=%async_computation.12 | async-start | bytes 1179648 | tf_op jit(solution)/shard_map/reduce_scatter | solution.py:12
  432.6 1.2 copy-start.1
  517.7 48.0 %copy-start.3 = (f32[256,512]{1,0:T(8,128)S(1)}, f32[256,512]{1,0:T(8,128)}, u32[]{:S(2)}) copy-start(f32[256,512]{1,0:T(8,128)} %all-reduce.14.cloned.1.call-done) | copy-start | bytes 1572868
  567.6 1.2 copy-start.10
  570.9 106.1 %all-gather.9.cloned.1.call-start = ((), (), s32[]{:S(2)}) async-start(), calls=%async_computation.13 | async-start | bytes 1179648 | tf_op jit(solution)/shard_map/all_gather | solution.py:50
  635.7 77.5 %all-reduce.20.cloned.1.call-start = ((), (), s32[]{:S(2)}) async-start(), calls=%async_computation.14 | async-start | bytes 1048576 | tf_op jit(solution)/shard_map/psum | solution.py:66
  681.0 101.1 %reduce-scatter.11.cloned.1.call-start = ((), (), s32[]{:S(2)}) async-start(), calls=%async_computation.15 | async-start | bytes 1179648 | tf_op jit(solution)/shard_map/reduce_scatter | solution.py:12
  716.3 65.7 %copy-start.4 = (f32[64,512]{1,0:T(8,128)S(1)}, f32[64,512]{1,0:T(8,128)}, u32[]{:S(2)}) copy-start(f32[64,512]{1,0:T(8,128)} %reduce-scatter.9.cloned.1.call-done) | copy-start | bytes 393220
  716.4 107.6 %all-gather.11.cloned.1.call-start = ((), (), s32[]{:S(2)}) async-start(), calls=%async_computation.16 | async-start | bytes 1179648 | tf_op jit(solution)/shard_map/all_gather | solution.py:50
  783.7 75.2 %all-reduce.22.cloned.1.call-start = ((), (), s32[]{:S(2)}) async-start(), calls=%async_computation.17 | async-start | bytes 1048576 | tf_op jit(solution)/shard_map/psum | solution.py:17
  825.9 36.1 %copy-start.6 = (f32[512,512]{1,0:T(8,128)S(1)}, f32[512,512]{1,0:T(8,128)}, u32[]{:S(2)}) copy-start(f32[512,512]{1,0:T(8,128)} %all-gather.11.cloned.1.call-done) | copy-start | bytes 3145732
  825.9 115.5 %all-reduce.24.cloned.1.call-start = ((), (), s32[]{:S(2)}) async-start(), calls=%async_computation.18 | async-start | bytes 2097152 | tf_op jit(solution)/shard_map/psum | solution.py:85
  861.9 124.3 %all-reduce.28.cloned.1.call-start = ((), (), s32[]{:S(2)}) async-start(), calls=%async_computation.20 | async-start | bytes 3145728 | tf_op jit(solution)/shard_map/psum | solution.py:85
  941.4 313.5 %all-reduce.26.cloned.1.call-start = ((), (), s32[]{:S(2)}) async-start(), calls=%async_computation.19 | async-start | bytes 2097152 | tf_op jit(solution)/shard_map/psum | solution.py:86
  987.5 1.2 copy-start
  1073.1 47.7 %copy-start.7 = (f32[256,512]{1,0:T(8,128)S(1)}, f32[256,512]{1,0:T(8,128)}, u32[]{:S(2)}) copy-start(f32[256,512]{1,0:T(8,128)} %get-tuple-element.69) | copy-start | bytes 1572868
  1120.8 1.1 copy-start.2
Sparse Core Ops, SparseCore 0:
  22.1 65.0 reduce-scatter.4
  89.4 39.2 all-gather.4
  132.7 32.0 all-reduce.11
  168.7 64.9 reduce-scatter.6
  236.2 39.1 all-gather.6
  278.2 32.0 all-reduce.13
  314.5 78.4 all-reduce.15
  395.3 35.8 all-reduce.17
  571.0 64.6 reduce-scatter.8
  637.7 39.2 all-gather.8
  681.1 32.0 all-reduce.19
  717.1 64.9 reduce-scatter.10
  784.8 39.1 all-gather.10
  826.8 32.1 all-reduce.21
  862.8 78.4 all-reduce.23
  943.7 42.4 all-reduce.27
  1124.1 130.7 all-reduce.25
